TPU v7x, 32 devices: a whole 2x2x4 slice. The times are simulated.
32 devices in a mesh: section: 4 (over y, x), dp: 8 (over z, core).
Axes of the slice: x: 2, y: 2, z: 4, core: 2. Of those that a mesh axis runs over, the one named last changes fastest.
Arguments:
- descriptors: bfloat16 [4, 4096, 1024], P(None, 'dp'), may hold values from -6 to 6
- layer_weight: bfloat16 [4, 8, 1024, 1024], P('section', None, 'dp'), may hold values from -0.25 to 0.25
- layer_bias: float32 [4, 8, 1024], P('section'), may hold values from -3 to 3
- readout: float32 [8, 1024], replicated, may hold values from -0.75 to 0.75
- self_energy: float32 [8], replicated, may hold values from -2 to -0.5
- tile_species: int32 [4, 32], P(None, 'dp'), may hold values from 0 to 7
- tile_fill: int32 [4, 32], P(None, 'dp'), may hold values from 1 to 128
Outputs:
- atom_energy: float32 [4, 4096], P('section', 'dp')
- energy: float32 [4], replicated
All inputs are finite; a program needn't handle non-finite values.
Results may differ from a plain program's by a relative error of at most 0.0044.
Values may be sent and summed in bfloat16 or wider, within the bound.
No kernel may reach another device: no remote copies, remote signals or barrier semaphores. Data moves between devices by JAX's collectives and lax.ppermute only.
A program may use at most 128 MiB of HBM per device.

v0:
```python
import jax
import jax.numpy as jnp
from jax import lax
from jax.sharding import PartitionSpec as P


def shifted(block, axis, distance):
    devices = range(lax.axis_size(axis))
    route = [(i - distance, i) for i in devices if i - distance in devices]
    return lax.ppermute(block, axis, route)


def smooth_unit(value):
    return jnp.maximum(value, 0.0) + jnp.minimum(jnp.expm1(jnp.minimum(value, 0.0)), 0.0)


def grouped_product(source, weights, species):
    chosen = jnp.take(weights, species, axis=0)
    return jnp.einsum("tai,tio->tao", source, chosen, preferred_element_type=jnp.float32)


def table_rows(onehot, table):
    return jnp.dot(onehot, table, precision=lax.Precision.HIGHEST)


def shards(descriptors, layer_weight, layer_bias, readout, self_energy, tile_species, tile_fill):
    sections = lax.axis_size("section")
    position = lax.axis_index("section")
    batches, atoms_dev, width = descriptors.shape
    tiles_dev = tile_species.shape[1]
    tile = atoms_dev // tiles_dev
    kinds = readout.shape[0]
    atoms_all = atoms_dev * lax.axis_size("dp")
    total_steps = batches + sections - 1
    bias = layer_bias[0]
    is_last = position == sections - 1
    kind_ids = jnp.arange(kinds, dtype=jnp.int32)
    slot_ids = jnp.arange(tile, dtype=jnp.int32)
    incoming = jnp.zeros((atoms_dev, width), jnp.bfloat16)
    stored = jnp.zeros((batches, atoms_dev), jnp.float32)
    energies = jnp.zeros((batches,), jnp.float32)
    weights = None
    for step in range(total_steps):
        batch = step - position
        valid = jnp.logical_and(batch >= 0, batch < batches)
        keep = jnp.logical_and(valid, is_last)
        index = jnp.clip(batch, 0, batches - 1)
        species = lax.dynamic_index_in_dim(tile_species, index, 0, keepdims=False)
        fill = lax.dynamic_index_in_dim(tile_fill, index, 0, keepdims=False)
        first = descriptors[min(step, batches - 1)]
        source = jnp.where(position == 0, first, incoming).reshape(tiles_dev, tile, width)
        if step == 0:
            weights = lax.all_gather(layer_weight[0], "dp", axis=1, tiled=True)
            product = grouped_product(source, weights, species)
        else:
            product = grouped_product(source, weights, species)
        onehot = (species[:, None] == kind_ids[None, :]).astype(jnp.float32)
        active = smooth_unit(product + table_rows(onehot, bias)[:, None, :])
        readout_rows = table_rows(onehot, readout)
        offsets = table_rows(onehot, self_energy[:, None])
        values = jnp.sum(active * readout_rows[:, None, :], axis=-1) + offsets
        present = slot_ids[None, :] < fill[:, None]
        values = jnp.where(jnp.logical_and(present, keep), values, jnp.float32(0.0)).reshape(
            atoms_dev
        )
        stored = stored.at[index].add(values)
        term = jnp.sum(values) / atoms_all
        finished = step - (sections - 1)
        if 0 <= finished < batches:
            energies = energies.at[finished].set(lax.psum(term, ("section", "dp")))
        if step < total_steps - 1:
            incoming = shifted(active.astype(jnp.bfloat16).reshape(atoms_dev, width), "section", 1)
    received = lax.all_to_all(stored, "section", split_axis=0, concat_axis=0, tiled=True)
    mine = received[sections - 1]
    return (mine[None, :], energies)


def solution(mesh):
    placed = (
        P(None, "dp", None),
        P("section", None, "dp", None),
        P("section", None, None),
        P(),
        P(),
        P(None, "dp"),
        P(None, "dp"),
    )
    return jax.shard_map(
        shards, mesh=mesh, in_specs=placed, out_specs=(P("section", "dp"), P()), check_vma=False
    )
```

profile of v0, /device:TPU:12, one launch (start us, length us, event | category | flops | bytes accessed | tf_op | source)
XLA Modules:
  0.0 464.9 jit_solution(16702947367663745943)
XLA Ops:
  12.9 146.2 %all-gather.3.cloned.1.call-done = bf16[1,8,1024,1024]{3,2,1,0:T(8,128)(2,1)} async-done(((bf16[1,8,128,1024]{3,2,1,0:T(8,128)(2,1)}), bf16[1,8,1024,1024]{3,2,1,0:T(8,128)(2,1)}) %all-gather.3.cloned.1.call-update) | async-done | bytes 16777232 | tf_op jit(solution)/shard_map/all_gather | solution.py:53
  159.1 11.7 %fusion.131 = (bf16[8,512,1024]{2,1,0:T(8,128)(2,1)}, bf16[8,512,1024]{2,1,0:T(8,128)(2,1)}) fusion(bf16[8,1024,1024]{2,1,0:T(8,128)(2,1)} %bitcast.146), kind=kLoop, calls=%fused_computation.259 | loop fusion | bytes 33554432 | tf_op jit(solution)/shard_map/jit(_take)/gather | solution.py:18
  170.8 6.2 %gather_fusion = bf16[4,512,1024]{2,1,0:T(8,128)(2,1)} fusion(bf16[8,512,1024]{2,1,0:T(8,128)(2,1)} %get-tuple-element.168, s32[1024]{0:T(1024)S(1)} %pad_clamp_fusion.6), kind=kCustom, calls=%fused_computation.clone | custom fusion | bytes 8388624 | tf_op jit(solution)/shard_map/jit(_take)/gather | solution.py:18
  176.9 6.1 %gather_fusion.1 = bf16[4,512,1024]{2,1,0:T(8,128)(2,1)} fusion(bf16[8,512,1024]{2,1,0:T(8,128)(2,1)} %get-tuple-element.169, s32[1024]{0:T(1024)S(1)} %pad_clamp_fusion.6), kind=kCustom, calls=%fused_computation.1.clone | custom fusion | bytes 8388624 | tf_op jit(solution)/shard_map/jit(_take)/gather | solution.py:18
  193.5 6.2 %gather_fusion.2 = bf16[4,512,1024]{2,1,0:T(8,128)(2,1)} fusion(bf16[8,512,1024]{2,1,0:T(8,128)(2,1)} %get-tuple-element.168, s32[1024]{0:T(1024)S(1)} %pad_clamp_fusion.5), kind=kCustom, calls=%fused_computation.2.clone | custom fusion | bytes 8388624 | tf_op jit(solution)/shard_map/jit(_take)/gather | solution.py:18
  199.7 6.1 %gather_fusion.3 = bf16[4,512,1024]{2,1,0:T(8,128)(2,1)} fusion(bf16[8,512,1024]{2,1,0:T(8,128)(2,1)} %get-tuple-element.169, s32[1024]{0:T(1024)S(1)} %pad_clamp_fusion.5), kind=kCustom, calls=%fused_computation.3.clone | custom fusion | bytes 8388624 | tf_op jit(solution)/shard_map/jit(_take)/gather | solution.py:18
  205.8 10.8 %collective-permute-done = bf16[512,1024]{1,0:T(8,128)(2,1)S(1)} collective-permute-done((bf16[512,1024]{1,0:T(8,128)(2,1)S(1)}, bf16[512,1024]{1,0:T(8,128)(2,1)S(1)}, u32[]{:S(2)}, u32[]{:S(2)}) %collective-permute-start) | collective-permute-done | bytes 1048608 | tf_op jit(solution)/shard_map/ppermute | solution.py:10
  217.9 5.4 %fusion.136 = (bf16[4,128,1024]{2,1,0:T(8,128)(2,1)S(1)}, f32[4,128]{1,0:T(4,128)S(1)}) fusion(f32[4,1024]{1,0:T(4,128)S(1)} %fusion.55, f32[4,1024]{1,0:T(4,128)S(1)} %fusion.45, bf16[4,128,1024]{2,1,0:T(8,128)(2,1)S(1)} %bitcast.148, bf16[4,512,1024]{2,1,0:T(8,128)(2,1)} %gather_fusion.3, bf16[4,512,1024]{2,1,0:T(8,128)(2,1)} %gather_fusion.2, ...), kind=kOutput, calls=%fused_computation.264 | convolution fusion | flops 1098907136 | bytes 10520580 | tf_op jit(solution)/shard_map/tai,tio->tao/dot_general | solution.py:19
  227.0 6.2 %gather_fusion.4 = bf16[4,512,1024]{2,1,0:T(8,128)(2,1)} fusion(bf16[8,512,1024]{2,1,0:T(8,128)(2,1)} %get-tuple-element.168, s32[1024]{0:T(1024)S(1)} %pad_clamp_fusion.4), kind=kCustom, calls=%fused_computation.4.clone | custom fusion | bytes 8388624 | tf_op jit(solution)/shard_map/jit(_take)/gather | solution.py:18
  233.2 6.1 %gather_fusion.5 = bf16[4,512,1024]{2,1,0:T(8,128)(2,1)} fusion(bf16[8,512,1024]{2,1,0:T(8,128)(2,1)} %get-tuple-element.169, s32[1024]{0:T(1024)S(1)} %pad_clamp_fusion.4), kind=kCustom, calls=%fused_computation.5.clone | custom fusion | bytes 8388624 | tf_op jit(solution)/shard_map/jit(_take)/gather | solution.py:18
  239.4 11.2 %collective-permute-done.1 = bf16[512,1024]{1,0:T(8,128)(2,1)S(1)} collective-permute-done((bf16[512,1024]{1,0:T(8,128)(2,1)S(1)}, bf16[512,1024]{1,0:T(8,128)(2,1)S(1)}, u32[]{:S(2)}, u32[]{:S(2)}) %collective-permute-start.1) | collective-permute-done | bytes 1048608 | tf_op jit(solution)/shard_map/ppermute | solution.py:10
  260.3 6.2 %gather_fusion.6 = bf16[4,512,1024]{2,1,0:T(8,128)(2,1)} fusion(bf16[8,512,1024]{2,1,0:T(8,128)(2,1)} %get-tuple-element.168, s32[1024]{0:T(1024)S(1)} %pad_clamp_fusion.3), kind=kCustom, calls=%fused_computation.6.clone | custom fusion | bytes 8388624 | tf_op jit(solution)/shard_map/jit(_take)/gather | solution.py:18
  266.5 6.1 %gather_fusion.7 = bf16[4,512,1024]{2,1,0:T(8,128)(2,1)} fusion(bf16[8,512,1024]{2,1,0:T(8,128)(2,1)} %get-tuple-element.169, s32[1024]{0:T(1024)S(1)} %pad_clamp_fusion.3), kind=kCustom, calls=%fused_computation.7.clone | custom fusion | bytes 8388624 | tf_op jit(solution)/shard_map/jit(_take)/gather | solution.py:18
  272.6 11.2 %collective-permute-done.2 = bf16[512,1024]{1,0:T(8,128)(2,1)S(1)} collective-permute-done((bf16[512,1024]{1,0:T(8,128)(2,1)S(1)}, bf16[512,1024]{1,0:T(8,128)(2,1)S(1)}, u32[]{:S(2)}, u32[]{:S(2)}) %collective-permute-start.2) | collective-permute-done | bytes 1048608 | tf_op jit(solution)/shard_map/ppermute | solution.py:10
  285.1 5.4 %fusion.134 = (bf16[4,128,1024]{2,1,0:T(8,128)(2,1)S(1)}, f32[4,128]{1,0:T(4,128)S(1)}) fusion(f32[4,1024]{1,0:T(4,128)S(1)} %fusion.53, f32[4,1024]{1,0:T(4,128)S(1)} %fusion.41, bf16[4,128,1024]{2,1,0:T(8,128)(2,1)S(1)} %bitcast.150, bf16[4,512,1024]{2,1,0:T(8,128)(2,1)} %gather_fusion.7, bf16[4,512,1024]{2,1,0:T(8,128)(2,1)} %gather_fusion.6, ...), kind=kOutput, calls=%fused_computation.262 | convolution fusion | flops 1098907136 | bytes 10520580 | tf_op jit(solution)/shard_map/tai,tio->tao/dot_general | solution.py:19
  293.5 6.3 %gather_fusion.8 = bf16[4,512,1024]{2,1,0:T(8,128)(2,1)} fusion(bf16[8,512,1024]{2,1,0:T(8,128)(2,1)} %get-tuple-element.168, s32[1024]{0:T(1024)S(1)} %pad_clamp_fusion.2), kind=kCustom, calls=%fused_computation.8.clone | custom fusion | bytes 8388624 | tf_op jit(solution)/shard_map/jit(_take)/gather | solution.py:18
  299.8 6.1 %gather_fusion.9 = bf16[4,512,1024]{2,1,0:T(8,128)(2,1)} fusion(bf16[8,512,1024]{2,1,0:T(8,128)(2,1)} %get-tuple-element.169, s32[1024]{0:T(1024)S(1)} %pad_clamp_fusion.2), kind=kCustom, calls=%fused_computation.9.clone | custom fusion | bytes 8388624 | tf_op jit(solution)/shard_map/jit(_take)/gather | solution.py:18
  305.9 6.2 %gather_fusion.10 = bf16[4,512,1024]{2,1,0:T(8,128)(2,1)} fusion(bf16[8,512,1024]{2,1,0:T(8,128)(2,1)} %get-tuple-element.168, s32[1024]{0:T(1024)S(1)} %pad_clamp_fusion.1), kind=kCustom, calls=%fused_computation.10.clone | custom fusion | bytes 8388624 | tf_op jit(solution)/shard_map/jit(_take)/gather | solution.py:18
  312.1 6.2 %gather_fusion.11 = bf16[4,512,1024]{2,1,0:T(8,128)(2,1)} fusion(bf16[8,512,1024]{2,1,0:T(8,128)(2,1)} %get-tuple-element.169, s32[1024]{0:T(1024)S(1)} %pad_clamp_fusion.1), kind=kCustom, calls=%fused_computation.11.clone | custom fusion | bytes 8388624 | tf_op jit(solution)/shard_map/jit(_take)/gather | solution.py:18
  318.2 6.1 %gather_fusion.12 = bf16[4,512,1024]{2,1,0:T(8,128)(2,1)} fusion(bf16[8,512,1024]{2,1,0:T(8,128)(2,1)} %get-tuple-element.168, s32[1024]{0:T(1024)S(1)} %pad_clamp_fusion), kind=kCustom, calls=%fused_computation.12.clone | custom fusion | bytes 8388624 | tf_op jit(solution)/shard_map/jit(_take)/gather | solution.py:18
  324.4 6.2 %gather_fusion.13 = bf16[4,512,1024]{2,1,0:T(8,128)(2,1)} fusion(bf16[8,512,1024]{2,1,0:T(8,128)(2,1)} %get-tuple-element.169, s32[1024]{0:T(1024)S(1)} %pad_clamp_fusion), kind=kCustom, calls=%fused_computation.13.clone | custom fusion | bytes 8388624 | tf_op jit(solution)/shard_map/jit(_take)/gather | solution.py:18
  342.2 21.4 %collective-permute-done.4 = bf16[512,1024]{1,0:T(8,128)(2,1)S(1)} collective-permute-done((bf16[512,1024]{1,0:T(8,128)(2,1)S(1)}, bf16[512,1024]{1,0:T(8,128)(2,1)S(1)}, u32[]{:S(2)}, u32[]{:S(2)}) %collective-permute-start.4) | collective-permute-done | bytes 1048608 | tf_op jit(solution)/shard_map/ppermute | solution.py:10
  376.3 18.7 %collective-permute-done.5 = bf16[512,1024]{1,0:T(8,128)(2,1)S(1)} collective-permute-done((bf16[512,1024]{1,0:T(8,128)(2,1)S(1)}, bf16[512,1024]{1,0:T(8,128)(2,1)S(1)}, u32[]{:S(2)}, u32[]{:S(2)}) %collective-permute-start.5) | collective-permute-done | bytes 1048608 | tf_op jit(solution)/shard_map/ppermute | solution.py:10
  409.5 45.5 %all-reduce.1 = (f32[1]{0:T(128)}, f32[1]{0:T(128)}, f32[1]{0:T(128)}, f32[1]{0:T(128)}) all-reduce(f32[1]{0:T(128)} %bitcast.62, f32[1]{0:T(128)} %bitcast.63, f32[1]{0:T(128)} %bitcast.64, f32[1]{0:T(128)} %bitcast.65), channel_id=1, replica_groups=mesh['section'=4,'dp'=8] {'section','dp'}, use_global_device_ids=true, to_apply=%region_15.17 | all-reduce | flops 4 | bytes 32 | tf_op jit(solution)/shard_map/psum | solution.py:70
  (97 shorter events, 74.2 us)
Async XLA Ops:
  7.2 3.3 copy-start
  7.2 151.9 %all-gather.3.cloned.1.call-start = ((), (), s32[]{:S(2)}) async-start(), calls=%async_computation.1 | async-start | bytes 18874368 | tf_op jit(solution)/shard_map/all_gather | solution.py:53
  183.1 8.8 %copy-start.2 = (s32[2]{0:T(128)S(1)}, s32[2]{0:T(128)}, u32[]{:S(2)}) copy-start(s32[2]{0:T(128)} %constant.301.clone.1) | copy-start | bytes 28
  183.1 9.6 %copy-start.4 = (f32[8]{0:T(128)S(1)}, f32[8]{0:T(128)}, u32[]{:S(2)}) copy-start(f32[8]{0:T(128)} %param.35) | copy-start | bytes 100
  183.1 10.2 %copy-start.3 = (f32[8,1024]{1,0:T(8,128)S(1)}, f32[8,1024]{1,0:T(8,128)}, u32[]{:S(2)}) copy-start(f32[8,1024]{1,0:T(8,128)} %param.34) | copy-start | bytes 98308
  188.5 28.1 %collective-permute-start = (bf16[512,1024]{1,0:T(8,128)(2,1)S(1)}, bf16[512,1024]{1,0:T(8,128)(2,1)S(1)}, u32[]{:S(2)}, u32[]{:S(2)}) collective-permute-start(bf16[512,1024]{1,0:T(8,128)(2,1)S(1)} %bitcast.164), channel_id=1, source_target_pairs={{0,8},{8,16},{16,24},{1,9},{9,17},{17,25},{2,10},{10,18},{18,26},{... | collective-permute-start | bytes 3145736 | tf_op jit(solution)/shard_map/ppermute | solution.py:10
  223.3 27.3 %collective-permute-start.1 = (bf16[512,1024]{1,0:T(8,128)(2,1)S(1)}, bf16[512,1024]{1,0:T(8,128)(2,1)S(1)}, u32[]{:S(2)}, u32[]{:S(2)}) collective-permute-start(bf16[512,1024]{1,0:T(8,128)(2,1)S(1)} %bitcast.166), channel_id=1, source_target_pairs={{0,8},{8,16},{16,24},{1,9},{9,17},{17,25},{2,10},{10,18},{18,26},{... | collective-permute-start | bytes 3145736 | tf_op jit(solution)/shard_map/ppermute | solution.py:10
  257.4 26.4 %collective-permute-start.2 = (bf16[512,1024]{1,0:T(8,128)(2,1)S(1)}, bf16[512,1024]{1,0:T(8,128)(2,1)S(1)}, u32[]{:S(2)}, u32[]{:S(2)}) collective-permute-start(bf16[512,1024]{1,0:T(8,128)(2,1)S(1)} %bitcast.165), channel_id=1, source_target_pairs={{0,8},{8,16},{16,24},{1,9},{9,17},{17,25},{2,10},{10,18},{18,26},{... | collective-permute-start | bytes 3145736 | tf_op jit(solution)/shard_map/ppermute | solution.py:10
  285.1 7.5 %copy-start.1 = (s32[4,4]{1,0:T(4,128)S(1)}, s32[4,4]{1,0:T(4,128)}, u32[]{:S(2)}) copy-start(s32[4,4]{1,0:T(4,128)} %param.37) | copy-start | bytes 196
  290.5 40.7 %collective-permute-start.3 = (bf16[512,1024]{1,0:T(8,128)(2,1)S(1)}, bf16[512,1024]{1,0:T(8,128)(2,1)S(1)}, u32[]{:S(2)}, u32[]{:S(2)}) collective-permute-start(bf16[512,1024]{1,0:T(8,128)(2,1)S(1)} %bitcast.161), channel_id=1, source_target_pairs={{0,8},{8,16},{16,24},{1,9},{9,17},{17,25},{2,10},{10,18},{18,26},{... | collective-permute-start | bytes 3145736 | tf_op jit(solution)/shard_map/ppermute | solution.py:10
  338.0 25.6 %collective-permute-start.4 = (bf16[512,1024]{1,0:T(8,128)(2,1)S(1)}, bf16[512,1024]{1,0:T(8,128)(2,1)S(1)}, u32[]{:S(2)}, u32[]{:S(2)}) collective-permute-start(bf16[512,1024]{1,0:T(8,128)(2,1)S(1)} %bitcast.163), channel_id=1, source_target_pairs={{0,8},{8,16},{16,24},{1,9},{9,17},{17,25},{2,10},{10,18},{18,26},{... | collective-permute-start | bytes 3145736 | tf_op jit(solution)/shard_map/ppermute | solution.py:10
  370.4 24.7 %collective-permute-start.5 = (bf16[512,1024]{1,0:T(8,128)(2,1)S(1)}, bf16[512,1024]{1,0:T(8,128)(2,1)S(1)}, u32[]{:S(2)}, u32[]{:S(2)}) collective-permute-start(bf16[512,1024]{1,0:T(8,128)(2,1)S(1)} %bitcast.162), channel_id=1, source_target_pairs={{0,8},{8,16},{16,24},{1,9},{9,17},{17,25},{2,10},{10,18},{18,26},{... | collective-permute-start | bytes 3145736 | tf_op jit(solution)/shard_map/ppermute | solution.py:10
  403.7 53.8 %all-to-all-start = ((f32[4,1,512]{2,1,0:T(1,128)}), f32[4,1,512]{2,1,0:T(1,128)S(1)}, u32[]{:S(2)}, u32[]{:S(2)}) async-start(f32[4,1,512]{2,1,0:T(1,128)} %constant_dynamic-update-slice_fusion), calls=%async_computation | async-start | bytes 16384 | tf_op jit(solution)/shard_map/all_to_all | solution.py:73
  457.4 0.6 copy-start.5
Sparse Core Ops, SparseCore 0:
  9.6 149.4 all-gather.2
where the time goes:
time: 466 us; the launch traced here: 465 us
  waiting for transfers between devices  220 us (47%)
  local copies, waits for them, and re-layouts  102 us (22%)
  blocking collectives  45.5 us (10%)
  matrix products  42.8 us (9%)
  other arithmetic  20.5 us (4%)
  starting transfers between devices  17.1 us (4%)
  between operations  17 us (4%)
    all_gather x1, waiting for transfers between devices, shards(): weights = lax.all_gather(layer_weight[0], 'dp', axis=1, tiled=True)  146 us
    gather x15, local copies, waits for them, and re-layouts, grouped_product(): chosen = jnp.take(weights, species, axis=0)  97.9 us
    ppermute x6, waiting for transfers between devices, shifted(): return lax.ppermute(block, axis, route)  73.3 us
    psum x1, blocking collectives, shards(): energies = energies.at[finished].set(lax.psum(term, ('section', 'dp')))  45.5 us
    dot_general x7, matrix products, grouped_product(): jnp.einsum('tai,tio->tao', source, chosen, preferred_element_type=jnp.flo...  37.9 us
    ppermute x6, starting transfers between devices, shifted(): return lax.ppermute(block, axis, route)  13.7 us
  transfers between devices with their start and end apart: 8, of which 6 were waited for; matrix products, arithmetic and copies ran while one was open for 20% of the time, Pallas kernels for 0%

commit v1 on v0

v1 whole, which is shorter than its diff:
```python
import functools

import jax
import jax.numpy as jnp
from jax import lax
from jax.experimental import pallas as pl
from jax.experimental.pallas import tpu as pltpu
from jax.sharding import PartitionSpec as P

GROUP = 2
SPLIT = 256


def pair_groups(devices, lanes):
    return [list(range(start, start + lanes)) for start in range(0, devices, lanes)]


def line_groups(devices, lanes):
    return [list(range(lane, devices, lanes)) for lane in range(lanes)]


def network(
    kind_ref, species_ref, fill_ref, self_ref, bias_ref, readout_ref, weight_hbm, *rest, sources, tile, layers
):
    tiles_hbm = rest[:sources]
    out_ref = rest[sources]
    weight, first, second, chosen, weight_sem, tile_sem = rest[sources + 1 :]
    positions, _, rows, width = weight_hbm.shape
    each = tiles_hbm[0].shape[0]
    kind = kind_ref[0]

    def weight_copy(layer, position):
        return pltpu.make_async_copy(
            weight_hbm.at[position, layer], weight.at[layer, pl.ds(position * rows, rows)], weight_sem.at[layer]
        )

    def tile_copy(source, index, slot):
        return pltpu.make_async_copy(
            tiles_hbm[source].at[index], first.at[pl.ds(slot * tile, tile)], tile_sem
        )

    count = jnp.int32(0)
    for source in range(sources):

        def pick(index, count, source=source):
            mine = species_ref[source * each + index] == kind

            @pl.when(mine)
            def _():
                chosen[count] = source * each + index
                tile_copy(source, index, count).start()

            return count + mine.astype(jnp.int32)

        count = lax.fori_loop(0, each, pick, count)
    for layer in range(layers):
        for position in range(positions):
            weight_copy(layer, position).start()
    out_ref[...] = jnp.zeros_like(out_ref)

    def settle(slot, carry):
        tile_copy(0, 0, slot).wait()
        return carry

    lax.fori_loop(0, count, settle, 0)
    groups = (count + GROUP - 1) // GROUP
    buffers = (first, second)
    for layer in range(layers):
        for position in range(positions):
            weight_copy(layer, position).wait()
        source, target = buffers[layer % 2], buffers[(layer + 1) % 2]
        is_last = layer == layers - 1

        def step(group, carry, layer=layer, source=source, target=target, is_last=is_last):
            begin = pl.multiple_of(group * (GROUP * tile), GROUP * tile)
            block = source[pl.ds(begin, GROUP * tile), :]
            sums = None
            for cut in range(0, width, SPLIT):
                value = jnp.dot(
                    block, weight[layer, :, cut : cut + SPLIT], preferred_element_type=jnp.float32
                )
                value = value + bias_ref[layer, :, cut : cut + SPLIT]
                active = jnp.maximum(value, jnp.exp(jnp.minimum(value, 0.0)) - 1.0)
                if not is_last:
                    target[pl.ds(begin, GROUP * tile), cut : cut + SPLIT] = active.astype(jnp.bfloat16)
                else:
                    terms = active * readout_ref[0, :, cut : cut + SPLIT]
                    for part in range(0, SPLIT, 128):
                        piece = terms[:, part : part + 128]
                        sums = piece if sums is None else sums + piece
            if is_last:
                for inner in range(GROUP):
                    slot = group * GROUP + inner
                    line = jnp.sum(sums[inner * tile : (inner + 1) * tile].T, axis=0, keepdims=True)
                    line = line + self_ref[0]

                    @pl.when(slot < count)
                    def _():
                        index = chosen[slot]
                        places = lax.broadcasted_iota(jnp.int32, (1, tile), 1)
                        out_ref[pl.ds(index, 1), :] = jnp.where(places < fill_ref[index], line, 0.0)

            return carry

        lax.fori_loop(0, groups, step, 0)


def energies_of(kind, species, fill, offset, bias, readout, weight, tile_sets):
    positions, layers, rows, width = weight.shape
    each, tile, _ = tile_sets[0].shape
    sources = len(tile_sets)
    slots = each * sources
    padded = -(-slots // GROUP) * GROUP
    smem = pl.BlockSpec(memory_space=pltpu.SMEM)
    vmem = pl.BlockSpec(memory_space=pltpu.VMEM)
    hbm = pl.BlockSpec(memory_space=pl.ANY)
    return pl.pallas_call(
        functools.partial(network, sources=sources, tile=tile, layers=layers),
        out_shape=jax.ShapeDtypeStruct((slots, tile), jnp.float32),
        in_specs=[smem, smem, smem, smem, vmem, vmem, hbm] + [hbm] * sources,
        out_specs=vmem,
        scratch_shapes=[
            pltpu.VMEM((layers, positions * rows, width), jnp.bfloat16),
            pltpu.VMEM((padded * tile, width), jnp.bfloat16),
            pltpu.VMEM((padded * tile, width), jnp.bfloat16),
            pltpu.SMEM((slots,), jnp.int32),
            pltpu.SemaphoreType.DMA((layers,)),
            pltpu.SemaphoreType.DMA,
        ],
        compiler_params=pltpu.CompilerParams(vmem_limit_bytes=56 * 1024 * 1024),
    )(kind, species, fill, offset, bias, readout, weight, *tile_sets)


def shards(descriptors, layer_weight, layer_bias, readout, self_energy, tile_species, tile_fill):
    sections = lax.axis_size("section")
    devices = lax.axis_size("dp")
    section = lax.axis_index("section")
    place = lax.axis_index("dp")
    batches, atoms_dev, width = descriptors.shape
    tiles_dev = tile_species.shape[1]
    tile = atoms_dev // tiles_dev
    kinds, rows = layer_weight.shape[1:3]
    lanes = kinds // sections
    positions = devices // lanes
    lane = place % lanes
    kind = section * lanes + lane
    pairs = pair_groups(devices, lanes)

    own = layer_weight[0].reshape(sections, lanes, rows, width)
    own = lax.all_to_all(own, "dp", 1, 1, tiled=True, axis_index_groups=pairs)
    own = lax.all_to_all(own, "section", 0, 0, tiled=True).reshape(sections, lanes * rows, width)
    weight = lax.all_gather(own, "dp", axis=0, axis_index_groups=line_groups(devices, lanes))

    bias = lax.all_gather(layer_bias[0], "section", axis=0)
    bias = lax.dynamic_index_in_dim(bias, kind, 1, keepdims=True)
    readout_row = lax.dynamic_index_in_dim(readout, kind, 0, keepdims=True)[None]
    offset = lax.dynamic_slice(self_energy, (kind,), (1,))

    table = jnp.stack([tile_species.reshape(-1), tile_fill.reshape(-1)])
    sets, tables = [], []
    mine = descriptors.reshape(batches * tiles_dev, tile, width)
    for turn in range(lanes):
        route = [(base[i], base[(i + turn) % lanes]) for base in pairs for i in range(lanes)]
        sets.append(lax.ppermute(mine, "dp", route) if turn else mine)
        tables.append(lax.ppermute(table, "dp", route) if turn else table)
    table = jnp.stack(tables, axis=1).reshape(2, -1)
    values = energies_of(kind[None], table[0], table[1], offset, bias, readout_row, weight, sets)
    values = values.reshape(lanes, batches, atoms_dev)
    partial = jnp.sum(values, axis=(0, 2)) / (atoms_dev * devices)

    order = (lane - jnp.arange(lanes)) % lanes
    values = jnp.take(values, order, axis=0)
    values = values.transpose(1, 0, 2)[:, None]
    here = (jnp.arange(positions) == place // lanes)[None, :, None, None]
    outgoing = jnp.where(here, values, 0.0)
    sums = jnp.broadcast_to(partial, outgoing.shape[:3] + (batches,))
    outgoing = jnp.concatenate([outgoing, sums], axis=-1).reshape(sections * devices, atoms_dev + batches)
    incoming = lax.all_to_all(outgoing, ("section", "dp"), 0, 0, tiled=True)
    total = jnp.sum(incoming, axis=0)
    return (total[None, :atoms_dev], total[atoms_dev:])


def solution(mesh):
    placed = (
        P(None, "dp", None),
        P("section", None, "dp", None),
        P("section", None, None),
        P(),
        P(),
        P(None, "dp"),
        P(None, "dp"),
    )
    return jax.shard_map(
        shards, mesh=mesh, in_specs=placed, out_specs=(P("section", "dp"), P()), check_vma=False
    )
```

time: 466 us -> 233 us (0.50)
  local copies, waits for them, and re-layouts: 102 us -> 8.52 us
  waiting for transfers between devices: 220 us -> 135 us
  matrix products: 42.8 us -> 0 us
  blocking collectives: 45.5 us -> 66.6 us
  other arithmetic: 20.5 us -> 0.43 us
  starting transfers between devices: 17.1 us -> 0.18 us
  Pallas kernels: 0 us -> 7.43 us
    gather x15 -> x1, local copies, waits for them, and re-layouts: 97.9 us -> 0.57 us  [shards(): values = jnp.take(values, order, axis=0)]
    ppermute x6 -> x2, waiting for transfers between devices: 73.3 us -> 0.01 us  [the longest x1 0.01 us: shards(): tables.append(lax.ppermute(table, 'dp', route) if turn else table)]
    all_to_all x0 -> x3, blocking collectives: none -> 58.5 us  [the longest x1 28.7 us: shards(): lax.all_to_all(own, 'section', 0, 0, tiled=True)]
    psum x1 -> x0, blocking collectives: 45.5 us -> none  [shards(): energies = energies.at[finished].set(lax.psum(term, ('section', 'dp')))]
    dot_general x28 -> x0, matrix products: 42.8 us -> none  [the longest x7 37.9 us: grouped_product(): jnp.einsum('tai,tio->tao', source, chosen, preferred_element_type=jnp.flo...]
    ppermute x6 -> x2, starting transfers between devices: 13.7 us -> 0.14 us  [the longest x1 0.07 us: shards(): sets.append(lax.ppermute(mine, 'dp', route) if turn else mine)]
    all_gather x1, waiting for transfers between devices: 146 us -> 135 us  [shards(): lax.all_gather(own, 'dp', axis=0, axis_index_groups=line_groups(devices,...]
    select_n x13 -> x3, other arithmetic: 9.49 us -> 0.16 us  [the longest x2 0.09 us: shards(): values = jnp.take(values, order, axis=0)]
  transfers between devices with their start and end apart: 8 -> 3, of which waited for: 6 -> 1; matrix products, arithmetic and copies ran while one was open for 20% -> 2% of each run, Pallas kernels for 0% -> 0%
where the time goes in v1:
time: 233 us; the launch traced here: 232 us
  waiting for transfers between devices  135 us (58%)
  blocking collectives  66.6 us (29%)
  between operations  14.2 us (6%)
  local copies, waits for them, and re-layouts  8.52 us (4%)
  Pallas kernels  7.43 us (3%)
    all_gather x1, waiting for transfers between devices, shards(): lax.all_gather(own, 'dp', axis=0, axis_index_groups=line_groups(devices,...  135 us
    all_to_all x1, blocking collectives, shards(): lax.all_to_all(own, 'section', 0, 0, tiled=True)  28.7 us
    all_to_all x1, blocking collectives, shards(): incoming = lax.all_to_all(outgoing, ('section', 'dp'), 0, 0, tiled=True)  24.4 us
    all_gather x1, blocking collectives, shards(): bias = lax.all_gather(layer_bias[0], 'section', axis=0)  8.04 us
    pallas_call x1, Pallas kernels, energies_of(): pl.pallas_call(functools.partial(network, sources=sources, tile=tile, lay...  7.43 us
    all_to_all x1, blocking collectives, shards(): own = lax.all_to_all(own, 'dp', 1, 1, tiled=True, axis_index_groups=pairs)  5.42 us
  transfers between devices with their start and end apart: 3, of which 1 were waited for; matrix products, arithmetic and copies ran while one was open for 2% of the time, Pallas kernels for 0%

profile of v1, /device:TPU:12, one launch (start us, length us, event | category | flops | bytes accessed | tf_op | source)
XLA Modules:
  0.0 232.2 jit_solution(47747834943407918)
XLA Ops:
  7.2 1.8 copy.12
  9.0 5.4 %all_to_all.19 = bf16[4,2,128,1024]{3,2,0,1:T(8,128)(2,1)S(1)} all-to-all(bf16[4,2,128,1024]{3,2,0,1:T(8,128)(2,1)S(1)} %copy.12), channel_id=1, replica_groups={{0,1},{2,3},{4,5},{6,7},{8,9},{10,11},{12,13},{14,15},{16,17},{18,19},{..., dimensions={1} | all-to-all | bytes 4194304 | tf_op jit(solution)/shard_map/all_to_all | solution.py:150
  14.4 0.2 copy.13
  14.6 28.7 %all_to_all.20 = bf16[4,2,128,1024]{3,2,1,0:T(8,128)(2,1)} all-to-all(bf16[4,2,128,1024]{3,2,1,0:T(8,128)(2,1)S(1)} %copy.13), channel_id=1, replica_groups=mesh['section'=4,'dp'=8] {'section'}, dimensions={0} | all-to-all | bytes 4194304 | tf_op jit(solution)/shard_map/all_to_all | solution.py:151
  43.3 0.1 collective-permute-start.1
  43.4 0.6 copy-done.2
  44.0 0.1 stack_reshape.7
  44.0 0.1 stack_reshape.6
  44.3 0.7 dynamic_slice.11.self_ref
  44.9 8.0 %all_gather.6 = f32[4,8,1024]{2,1,0:T(8,128)S(1)} all-gather(f32[1,8,1024]{2,1,0:T(8,128)S(1)} %copy-done.1), channel_id=1, replica_groups=mesh['section'=4,'dp'=8] {'section'}, dimensions={0}, use_global_device_ids=true | all-gather | bytes 163840 | tf_op jit(solution)/shard_map/all_gather | solution.py:154
  53.0 0.6 dynamic-slice_bitcast_fusion.readout_ref
  53.6 0.6 constant_dynamic-slice_fusion.bias_ref
  54.3 0.1 broadcast_in_dim.51
  54.4 0.6 squeeze.6.species_ref
  55.0 0.7 squeeze.7.fill_ref
  55.7 134.8 %all-gather.2.cloned.1.call-done.weight_hbm = bf16[4,4,256,1024]{3,2,1,0:T(8,128)(2,1)} async-done(((bf16[1,4,256,1024]{3,2,1,0:T(8,128)(2,1)}), bf16[4,4,256,1024]{3,2,1,0:T(8,128)(2,1)}) %all-gather.2.cloned.1.call-update) | async-done | bytes 8388624 | tf_op jit(solution)/shard_map/all_gather | solution.py:152
  190.5 7.4 %shard_map.86 = f32[32,128]{1,0:T(8,128)} custom-call(s32[1]{0:T(128)} %bitcast.kind_ref, s32[32]{0:T(128)} %squeeze.6.species_ref, s32[32]{0:T(128)} %squeeze.7.fill_ref, f32[1]{0:T(128)} %dynamic_slice.11.self_ref, f32[4,1,1024]{2,1,0:T(1,128)} %constant_dynamic-slice_fusion.bias_ref, f32[1,1,1024]{2,1,0:T(1,128)} %dynamic-slice_bitcast_fusion.readout_ref, ...), custom_call_target="tpu_custom_call" | custom-call | tf_op jit(solution)/shard_map/pallas_call | solution.py:117
  198.0 0.7 reshape.82
  198.7 0.6 gather_fusion
  199.3 0.1 select_bitcast_fusion
  199.4 0.1 reduce_sum.18
  199.7 24.4 %all_to_all.21 = f32[32,1,516]{2,1,0:T(1,128)S(1)} all-to-all(f32[32,1,516]{2,1,0:T(1,128)S(1)} %all_to_all.14), channel_id=1, replica_groups=mesh['section'=4,'dp'=8] {'section','dp'}, dimensions={0} | all-to-all | bytes 132096 | tf_op jit(solution)/shard_map/all_to_all | solution.py:178
  224.2 0.6 slice.16
  224.8 0.5 slice.17
  (30 shorter events, 0.6 us)
Async XLA Ops:
  7.2 45.8 %copy-start = (f32[8,1024]{1,0:T(8,128)S(1)}, f32[8,1024]{1,0:T(8,128)}, u32[]{:S(2)}) copy-start(f32[8,1024]{1,0:T(8,128)} %param.10) | copy-start | bytes 98308
  7.2 183.4 %all-gather.2.cloned.1.call-start = ((), (), s32[]{:S(2)}) async-start(), calls=%async_computation.3 | async-start | bytes 10485760 | tf_op jit(solution)/shard_map/all_gather | solution.py:152
  43.3 0.7 copy-start.2
  43.3 0.8 copy-start.3
  43.3 1.0 copy-start.4
  43.3 1.6 copy-start.1
  43.3 12.4 %collective-permute-start.1 = (bf16[16,128,1024]{2,1,0:T(8,128)(2,1)}, bf16[16,128,1024]{2,1,0:T(8,128)(2,1)}, u32[]{:S(2)}, u32[]{:S(2)}) collective-permute-start(bf16[16,128,1024]{2,1,0:T(8,128)(2,1)} %bitcast.15), channel_id=1, source_target_pairs={{0,1},{1,0},{2,3},{3,2},{4,5},{5,4},{6,7},{7,6},{8,9},{9,8},{10,11... | collective-permute-start | bytes 12582920 | tf_op jit(solution)/shard_map/ppermute | solution.py:164
  44.1 10.3 %collective-permute-start = (s32[2,16]{1,0:T(2,128)S(1)}, s32[2,16]{1,0:T(2,128)S(1)}, u32[]{:S(2)}, u32[]{:S(2)}) collective-permute-start(s32[2,16]{1,0:T(2,128)S(1)} %get-tuple-element.5), channel_id=1, source_target_pairs={{0,1},{1,0},{2,3},{3,2},{4,5},{5,4},{6,7},{7,6},{8,9},{9,8},{10,11... | collective-permute-start | bytes 392 | tf_op jit(solution)/shard_map/ppermute | solution.py:165
Sparse Core Ops, SparseCore 0:
  43.4 147.0 all-gather.1
